TPU v7x, 32 devices: a whole 2x2x4 slice. The times are simulated.
32 devices in a mesh: groups: 2 (over x), chol: 16 (over z, y, core).
Axes of the slice: x: 2, y: 2, z: 4, core: 2. Of those that a mesh axis runs over, the one named last changes fastest.
Arguments:
- green_rows: bfloat16 [128, 65536], P('groups', 'chol'), parts along dimension 0, may hold values from -6 to 6
- factors: bfloat16 [5120, 65536], P(None, 'chol'), may hold values from -0.03125 to 0.03125
- noise_draws: float32 [128, 5120], P('groups', 'chol'), parts along dimension 0, may hold values from -6 to 6
Outputs:
- potential: float32 [128, 65536], P('groups', 'chol'), parts along dimension 0
- log_weight: float32 [128], P(('groups', 'chol')), parts along dimension 0
There are 2 independent parts, one for each index of `groups`. A program takes and returns all parts, laid end to end along the dimension named above; an argument that names none is the same for every part. Nothing has to cross between parts.
All inputs are finite; a program needn't handle non-finite values.
Results may differ from a plain program's by a relative error of at most 0.0029.
Values may be sent and summed in bfloat16 or wider, within the bound.
A program may use at most 128 MiB of HBM per device.

v0:
```python
import functools
import math

import jax
import jax.numpy as jnp
from jax import lax
from jax.experimental import pallas as pl
from jax.experimental.pallas import tpu as pltpu
from jax.sharding import PartitionSpec as P

MESH = pl.DeviceIdType.MESH
STAGES = 4


def flip(a, b, bits):
    total = 0
    for bit in range(bits):
        x = lax.rem(lax.div(a, 2**bit), 2)
        y = lax.rem(lax.div(b, 2**bit), 2) if not isinstance(b, int) else (b >> bit) & 1
        total = total + (x + y - 2 * x * y) * 2**bit
    return total


def kernel(n, pack, green, factors, noise, pot, logw, fac, own, d2d_out, d2d_in, rs_in, ag, nz,
           lhs, lw, lws, fac_sem, ds, dr, rs, rr, gs, gr, fs, fr, ls, lr, ps, pr):
    chips = n // 2
    bits = chips.bit_length() - 1
    total = factors.shape[0]
    nv = total // n
    half = nv // pack
    walkers = green.shape[0]
    me = lax.axis_index("chol")
    chip, core = lax.div(me, 2), lax.rem(me, 2)
    other = 1 - core
    partner = chip * 2 + other

    def peer(k):
        return flip(chip, k, bits) * 2 + core

    def load(i):
        k = chips - 1 - i
        rows = pl.ds(pl.multiple_of(flip(chip, k, bits) * (2 * nv), 2 * nv), 2 * nv)
        return pltpu.make_async_copy(factors.at[rows, :], fac.at[rows, :], fac_sem.at[k])

    def start_load(i, c):
        load(i).start()
        return c

    lax.fori_loop(0, chips, start_load, 0)

    barrier = pltpu.get_barrier_semaphore()
    pl.semaphore_signal(barrier, inc=1, device_id={"chol": partner}, device_id_type=MESH)

    def greet(k, c):
        pl.semaphore_signal(barrier, inc=1, device_id={"chol": peer(k)}, device_id_type=MESH)
        return c

    lax.fori_loop(1, chips, greet, 0)
    turned = noise[...].T
    nz[...] = jnp.concatenate([turned[j * half:(j + 1) * half] for j in range(pack)], axis=1)
    pl.semaphore_wait(barrier, chips)

    def remote(src, dst, s, r, to):
        return pltpu.make_async_remote_copy(
            src_ref=src, dst_ref=dst, send_sem=s, recv_sem=r,
            device_id={"chol": to}, device_id_type=MESH)

    def d2d(k):
        return remote(d2d_out.at[k], d2d_in.at[k], ds.at[k], dr.at[k], partner)

    def scatter(k):
        return remote(own.at[k], rs_in.at[k], rs.at[k], rr.at[k], peer(k))

    def partial(k, which):
        base = (flip(chip, k, bits) * 2 + which) * nv
        parts = []
        for j in range(pack):
            rows = pl.ds(pl.multiple_of(base + j * half, 16), half)
            parts.append(lax.dot_general(fac[rows, :], green[...], (((1,), (1,)), ((), ())),
                                         preferred_element_type=jnp.float32))
        return jnp.concatenate(parts, axis=1) if pack > 1 else parts[0]

    def finish(k):
        d2d(k).wait_recv()
        own[k] = own[k] + d2d_in[k]

    def step(i, c):
        k = chips - 1 - i
        load(i).wait()
        d2d_out[k] = partial(k, other)
        d2d(k).start()

        @pl.when(i > 0)
        def _():
            finish(k + 1)
            scatter(k + 1).start()

        own[k] = partial(k, core)
        return c

    lax.fori_loop(0, chips, step, 0)
    finish(0)

    def gather_sum(k, acc):
        scatter(k).wait_recv()
        return acc + rs_in[k]

    forces = lax.fori_loop(1, chips, gather_sum, own[0])
    capped = jnp.tanh(forces)
    fields = nz[...] - capped

    def spread(k):
        mine = ag.at[0, core]
        return remote(mine, ag.at[k, core], gs.at[k], gr.at[k], peer(k))

    def forward(k):
        return remote(ag.at[k, core], ag.at[k, core], fs.at[k], fr.at[k], partner)

    def forward_in(k):
        return remote(ag.at[k, other], ag.at[k, other], fs.at[k], fr.at[k], partner)

    def tell(k):
        return remote(lw.at[0], lw.at[k], ls.at[k], lr.at[k], peer(k))

    pair_sum = remote(lws.at[0], lws.at[1], ps, pr, partner)

    ag[0, core] = fields.astype(jnp.bfloat16)
    forward(0).start()

    def start_spread(k, c):
        spread(k).start()
        return c

    lax.fori_loop(1, chips, start_spread, 0)
    row = jnp.sum(fields * capped - 0.5 * capped * capped, axis=0, keepdims=True)
    lw[0] = jnp.broadcast_to(row, lw.shape[1:])

    def start_tell(k, c):
        tell(k).start()
        return c

    lax.fori_loop(1, chips, start_tell, 0)

    per_stage = chips // STAGES
    deep = total // STAGES
    own_stage = lax.div(chip, per_stage)
    cols = pot.shape[1]
    width = min(512, cols // 2)
    halves = cols // 2 // width

    def pull(s):
        def one(k, c):
            spread(k).wait_recv()
            forward(k).start()
            return c
        lax.fori_loop(max(1, s * per_stage), (s + 1) * per_stage, one, 0)

    def settle(s):
        def one(k, c):
            forward_in(k).wait_recv()
            return c
        lax.fori_loop(s * per_stage, (s + 1) * per_stage, one, 0)

    pull(0)
    settle(0)
    for s in range(STAGES):
        plane = flip(own_stage, s, 2)
        blocks = []
        for m in range(per_stage):
            k = flip(plane * per_stage + m, chip, bits)
            for c in range(2):
                block = ag[k, c]
                for j in range(pack):
                    blocks.append(block[:, j * walkers:(j + 1) * walkers])
        lhs[...] = jnp.concatenate(blocks, axis=0).T
        rows = pl.ds(pl.multiple_of(plane * deep, deep), deep)

        def column(t, c, s=s, rows=rows):
            at = pl.ds(pl.multiple_of(t * width, width), width)
            value = jnp.dot(lhs[...], fac[rows, at], preferred_element_type=jnp.float32)
            pot[:, at] = value if s == 0 else pot[:, at] + value
            return c

        lax.fori_loop(0, halves, column, 0)
        if s + 1 < STAGES:
            pull(s + 1)
        if s == STAGES - 2:
            def add(k, acc):
                tell(k).wait_recv()
                return acc + lw[k]
            lws[0] = lax.fori_loop(1, chips, add, lw[0])
            pair_sum.start()
        lax.fori_loop(halves, 2 * halves, column, 0)
        if s + 1 < STAGES:
            settle(s + 1)

    pair_sum.wait()
    packed = lws[0, 0:1, :] + lws[1, 0:1, :]
    row = packed[:, 0:walkers]
    for j in range(1, pack):
        row = row + packed[:, j * walkers:(j + 1) * walkers]
    per = walkers // n
    lane = lax.broadcasted_iota(jnp.int32, (1, walkers), 1)
    spot = lax.broadcasted_iota(jnp.int32, (1, per), 1)
    mine = jnp.zeros((1, per), jnp.float32)
    for j in range(per):
        one = jnp.sum(jnp.where(lane == me * per + j, row, 0.0), axis=1, keepdims=True)
        mine = jnp.where(spot == j, one, mine)
    logw[...] = (mine / math.sqrt(total)).reshape(per)

    d2d(0).wait_send()
    forward(0).wait_send()

    def drain(k, c):
        d2d(k).wait_send()
        scatter(k).wait_send()
        spread(k).wait_send()
        forward(k).wait_send()
        tell(k).wait_send()
        return c

    lax.fori_loop(1, chips, drain, 0)


def solution(mesh):
    n = mesh.shape["chol"]

    def per_device(green, factors, noise):
        walkers, cols = green.shape
        total = factors.shape[0]
        chips = n // 2
        pack = max(1, 128 // walkers)
        half, lanes = total // n // pack, walkers * pack
        vmem = pl.BlockSpec(memory_space=pltpu.VMEM)
        dma = pltpu.SemaphoreType.DMA
        block = pltpu.VMEM((chips, half, lanes), jnp.float32)
        pot, logw = pl.pallas_call(
            functools.partial(kernel, n, pack),
            out_shape=(jax.ShapeDtypeStruct((walkers, cols), jnp.float32),
                       jax.ShapeDtypeStruct((walkers // n,), jnp.float32)),
            in_specs=[vmem, pl.BlockSpec(memory_space=pl.ANY), vmem],
            out_specs=(vmem, vmem),
            scratch_shapes=[
                pltpu.VMEM(factors.shape, jnp.bfloat16),
                block, block, block, block,
                pltpu.VMEM((chips, 2, half, lanes), jnp.bfloat16),
                pltpu.VMEM((half, lanes), jnp.float32),
                pltpu.VMEM((walkers, total // STAGES), jnp.bfloat16),
                pltpu.VMEM((chips, 8, lanes), jnp.float32),
                pltpu.VMEM((2, 8, lanes), jnp.float32),
            ] + [dma((chips,))] * 11 + [dma, dma],
            compiler_params=pltpu.CompilerParams(
                collective_id=0, has_side_effects=True, vmem_limit_bytes=67043328),
        )(green, factors, noise)
        return pot, logw

    return jax.shard_map(
        per_device,
        mesh=mesh,
        in_specs=(P("groups", "chol"), P(None, "chol"), P("groups", "chol")),
        out_specs=(P("groups", "chol"), P(("groups", "chol"))),
        check_vma=False,
    )
```

profile of v0, /device:TPU:0, one launch (start us, length us, event | category | flops | bytes accessed | tf_op | source)
XLA Modules:
  0.0 49.0 jit_solution(6838492071618620722)
XLA Ops:
  0.6 44.9 %shard_map.50 = (f32[64,4096]{1,0:T(8,128)}, f32[4]{0:T(128)}) custom-call(bf16[64,4096]{1,0:T(8,128)(2,1)} %green.1, bf16[5120,4096]{1,0:T(8,128)(2,1)} %factors.1, f32[64,320]{1,0:T(8,128)} %noise.1), custom_call_target="tpu_custom_call" | custom-call | tf_op jit(solution)/shard_map/pallas_call | solution.py:237
  45.6 2.3 %copy.7 = f32[64,4096]{1,0:T(8,128)} copy(f32[64,4096]{1,0:T(8,128)} %get-tuple-element.4) | data formatting | bytes 2097152
  47.9 1.1 %copy.8 = f32[4]{0:T(128)} copy(f32[4]{0:T(128)} %get-tuple-element.5) | data formatting | bytes 32
where the time goes:
time: 49.3 us; the launch traced here: 49 us
  Pallas kernels  44.9 us (91%)
  local copies, waits for them, and re-layouts  3.38 us (7%)
  between operations  0.64 us (1%)
    pallas_call x1, Pallas kernels, per_device(): pl.pallas_call(functools.partial(kernel, n, pack), out_shape=(jax.ShapeDt...  44.9 us
    unnamed x2, local copies, waits for them, and re-layouts  3.38 us

commit v1 on v0

--- a/solution.py
+++ b/solution.py
@@ -58,8 +58,6 @@
     lax.fori_loop(1, chips, greet, 0)
     turned = noise[...].T
     nz[...] = jnp.concatenate([turned[j * half:(j + 1) * half] for j in range(pack)], axis=1)
-    pl.semaphore_wait(barrier, chips)
-
     def remote(src, dst, s, r, to):
         return pltpu.make_async_remote_copy(
             src_ref=src, dst_ref=dst, send_sem=s, recv_sem=r,
@@ -90,15 +88,17 @@
         d2d_out[k] = partial(k, other)
         d2d(k).start()
 
-        @pl.when(i > 0)
-        def _():
-            finish(k + 1)
-            scatter(k + 1).start()
-
+        finish(k + 1)
+        scatter(k + 1).start()
         own[k] = partial(k, core)
         return c
 
-    lax.fori_loop(0, chips, step, 0)
+    load(0).wait()
+    d2d_out[chips - 1] = partial(chips - 1, other)
+    pl.semaphore_wait(barrier, chips)
+    d2d(chips - 1).start()
+    own[chips - 1] = partial(chips - 1, core)
+    lax.fori_loop(1, chips, step, 0)
     finish(0)
 
     def gather_sum(k, acc):
@@ -145,7 +145,7 @@
     deep = total // STAGES
     own_stage = lax.div(chip, per_stage)
     cols = pot.shape[1]
-    width = min(512, cols // 2)
+    width = cols // 2
     halves = cols // 2 // width
 
     def pull(s):

time: 49.3 us -> 45.7 us (0.927)
  Pallas kernels: 44.9 us -> 41.5 us
    pallas_call x1, Pallas kernels: 44.9 us -> 41.5 us  [per_device(): pl.pallas_call(functools.partial(kernel, n, pack), out_shape=(jax.ShapeDt...]
where the time goes in v1:
time: 45.7 us; the launch traced here: 45.5 us
  Pallas kernels  41.5 us (91%)
  local copies, waits for them, and re-layouts  3.38 us (7%)
  between operations  0.64 us (1%)
    pallas_call x1, Pallas kernels, per_device(): pl.pallas_call(functools.partial(kernel, n, pack), out_shape=(jax.ShapeDt...  41.5 us
    unnamed x2, local copies, waits for them, and re-layouts  3.38 us

profile of v1, /device:TPU:0, one launch (start us, length us, event | category | flops | bytes accessed | tf_op | source)
XLA Modules:
  0.0 45.5 jit_solution(3507683779721257587)
XLA Ops:
  0.6 41.5 %shard_map.50 = (f32[64,4096]{1,0:T(8,128)}, f32[4]{0:T(128)}) custom-call(bf16[64,4096]{1,0:T(8,128)(2,1)} %green.1, bf16[5120,4096]{1,0:T(8,128)(2,1)} %factors.1, f32[64,320]{1,0:T(8,128)} %noise.1), custom_call_target="tpu_custom_call" | custom-call | tf_op jit(solution)/shard_map/pallas_call | solution.py:237
  42.1 2.3 %copy.7 = f32[64,4096]{1,0:T(8,128)} copy(f32[64,4096]{1,0:T(8,128)} %get-tuple-element.4) | data formatting | bytes 2097152
  44.4 1.1 %copy.8 = f32[4]{0:T(128)} copy(f32[4]{0:T(128)} %get-tuple-element.5) | data formatting | bytes 32

commit v2 on v0

v2 whole, which is shorter than its diff:
```python
import functools
import math

import jax
import jax.numpy as jnp
from jax import lax
from jax.experimental import pallas as pl
from jax.experimental.pallas import tpu as pltpu
from jax.sharding import PartitionSpec as P

MESH = pl.DeviceIdType.MESH


def flip(a, b, bits):
    total = 0
    for bit in range(bits):
        x = lax.rem(lax.div(a, 2**bit), 2)
        y = lax.rem(lax.div(b, 2**bit), 2) if not isinstance(b, int) else (b >> bit) & 1
        total = total + (x + y - 2 * x * y) * 2**bit
    return total


def kernel(n, pack, waves, green, factors, noise, pot, logw,
           grn, nzi, fac, part, d2d_in, own, rs_in, far_out, far_in, ag, nz, lhs, lw, lws,
           in_sem, fac_sem, ds, dr, rs, rr, gs, gr, fs, fr, ls, lr, ps, pr):
    chips = n // 2
    bits = chips.bit_length() - 1
    pairs = chips // 2
    total, cols = factors.shape
    nv = total // n
    nw = nv // waves
    half = nw // pack
    walkers = green.shape[0]
    deep = 4 * nw
    me = lax.axis_index("chol")
    chip, core = lax.div(me, 2), lax.rem(me, 2)
    other = 1 - core
    partner = chip * 2 + other

    def peer(k):
        return flip(chip, k, bits) * 2 + core

    def at(w, k):
        return w * chips + k

    def base(w, p):
        return pl.multiple_of((w * pairs + p) * deep, deep)

    def load(w, p, b, c):
        src = (flip(chip, 2 * p + b, bits) * 2 + c) * nv + w * nw
        return pltpu.make_async_copy(
            factors.at[pl.ds(pl.multiple_of(src, nw), nw), :],
            fac.at[pl.ds(pl.multiple_of(base(w, p) + (2 * b + c) * nw, nw), nw), :],
            fac_sem.at[2 * b + c, w * pairs + p])

    green_in = pltpu.make_async_copy(green, grn, in_sem.at[0])
    noise_in = pltpu.make_async_copy(noise, nzi, in_sem.at[1])
    green_in.start()
    steps = waves * pairs

    def where(t):
        return lax.div(t, pairs), pairs - 1 - lax.rem(t, pairs)

    def start_load(t, c):
        w, p = where(t)
        for b in (0, 1):
            for e in range(2):
                load(w, p, b, e).start()
        return c

    start_load(0, 0)
    noise_in.start()
    lax.fori_loop(1, steps, start_load, 0)

    barrier = pltpu.get_barrier_semaphore()
    pl.semaphore_signal(barrier, inc=1, device_id={"chol": partner}, device_id_type=MESH)

    def greet(k, c):
        pl.semaphore_signal(barrier, inc=1, device_id={"chol": peer(k)}, device_id_type=MESH)
        return c

    lax.fori_loop(1, chips, greet, 0)

    def remote(src, dst, s, r, to):
        return pltpu.make_async_remote_copy(
            src_ref=src, dst_ref=dst, send_sem=s, recv_sem=r,
            device_id={"chol": to}, device_id_type=MESH)

    def d2d(w, k):
        q = at(w, k)
        return remote(part.at[q, other], d2d_in.at[q], ds.at[q], dr.at[q], partner)

    def near(w, k):
        q = at(w, k)
        return remote(own.at[q], rs_in.at[q], rs.at[q], rr.at[q], peer(k))

    def far(w, k):
        q = at(w, k)
        return remote(far_out.at[q], far_in.at[q], rs.at[q], rr.at[q], peer(k))

    def pack_rows(o):
        rows = [o[j * half:(j + 1) * half] for j in range(pack)]
        return jnp.concatenate(rows, axis=1) if pack > 1 else rows[0]

    def product(w, p):
        for b in range(2):
            for e in range(2):
                load(w, p, b, e).wait()
        o = lax.dot_general(fac[pl.ds(base(w, p), deep), :], grn[...], (((1,), (1,)), ((), ())),
                            preferred_element_type=jnp.float32)
        for b in range(2):
            for e in range(2):
                part[at(w, 2 * p + b), e] = pack_rows(o[(2 * b + e) * nw:(2 * b + e + 1) * nw])

    def swap(w, p):
        for b in (1, 0):
            d2d(w, 2 * p + b).start()

    def reduced(w, k):
        q = at(w, k)
        d2d(w, k).wait_recv()
        return part[q, core] + d2d_in[q]

    def send_near(w, k):
        own[at(w, k)] = reduced(w, k)
        near(w, k).start()

    def send_far(w, k):
        far_out[at(w, k)] = reduced(w, k).astype(jnp.bfloat16)
        far(w, k).start()

    def send_pair(w, p):
        @pl.when(p >= 2)
        def _():
            send_far(w, 2 * p + 1)
            send_far(w, 2 * p)

        @pl.when(p < 2)
        def _():
            send_near(w, 2 * p + 1)

        @pl.when(p == 1)
        def _():
            send_near(w, 2 * p)

        @pl.when(p == 0)
        def _():
            own[at(w, 0)] = reduced(w, 0)

    def direct(k):
        return k < 4 or k % 2 == 0

    def spread(w, k):
        return remote(ag.at[w, 0, core], ag.at[w, k, core], gs.at[w, k], gr.at[w, k], peer(k))

    def relay(w, k):
        return remote(ag.at[w, k - 1, core], ag.at[w, k, core], gs.at[w, k], gr.at[w, k], peer(1))

    def forward(w, k):
        return remote(ag.at[w, k, core], ag.at[w, k, core], fs.at[w, k], fr.at[w, k], partner)

    def forward_in(w, k):
        return remote(ag.at[w, k, other], ag.at[w, k, other], fs.at[w, k], fr.at[w, k], partner)

    def tell(k):
        return remote(lw.at[0], lw.at[k], ls.at[k], lr.at[k], peer(k))

    pair_sum = remote(lws.at[0], lws.at[1], ps, pr, partner)
    order = [p for p in (0, 1, 3, 2) if p < pairs] + list(range(4, pairs))

    def combine(w):
        def near_sum(k, acc):
            near(w, k).wait_recv()
            return acc + rs_in[at(w, k)]

        def far_sum(k, acc):
            far(w, k).wait_recv()
            return acc + far_in[at(w, k)].astype(jnp.float32)

        forces = lax.fori_loop(4, chips, far_sum, own[at(w, 0)])
        forces = lax.fori_loop(1, 4, near_sum, forces)
        capped = jnp.tanh(forces)
        fields = nz[w] - capped
        ag[w, 0, core] = fields.astype(jnp.bfloat16)
        forward(w, 0).start()
        for p in order:
            for k in (2 * p, 2 * p + 1):
                if k and direct(k):
                    spread(w, k).start()
        row = jnp.sum(fields * capped - 0.5 * capped * capped, axis=0, keepdims=True)
        row = jnp.broadcast_to(row, lw.shape[1:])
        lw[0] = row if w == 0 else lw[0] + row
        if w == waves - 1:
            def start_tell(k, c):
                tell(k).start()
                return c

            lax.fori_loop(1, chips, start_tell, 0)

    def pull(w, ks):
        for k in ks:
            spread(w, k).wait_recv()
            forward(w, k).start()
            if k >= 4 and k % 2 == 0:
                relay(w, k + 1).start()

    def settle(w, p):
        for k in (2 * p, 2 * p + 1):
            forward_in(w, k).wait_recv()

    def stage(w, p):
        blocks = []
        for k in (2 * p, 2 * p + 1):
            for e in range(2):
                block = ag[w, k, e]
                for j in range(pack):
                    blocks.append(block[:, j * walkers:(j + 1) * walkers])
        lhs[...] = jnp.concatenate(blocks, axis=0).T
        value = jnp.dot(lhs[...], fac[pl.ds(base(w, p), deep), :], preferred_element_type=jnp.float32)
        pot[...] = value if w == 0 and p == order[0] else pot[...] + value

    green_in.wait()

    def step(t, c):
        w, p = where(t)
        product(w, p)

        @pl.when(t == 0)
        def _():
            pl.semaphore_wait(barrier, chips)

        swap(w, p)

        @pl.when(t > 0)
        def _():
            send_pair(*where(t - 1))

        @pl.when(t == 0)
        def _():
            noise_in.wait()
            turned = nzi[...].T
            for v in range(waves):
                nz[v] = pack_rows(turned[v * nw:(v + 1) * nw])

        for v in range(waves - 1):
            @pl.when(t == (v + 1) * pairs + 1)
            def _(v=v):
                combine(v)
        return c

    lax.fori_loop(0, steps, step, 0)
    evens = [k for p in order[2:] for k in (2 * p,)]
    odds = [k + 1 for k in evens]
    if waves == 1:
        send_pair(0, 0)
        combine(0)
    for w in range(waves):
        last = w == waves - 1
        pull(w, [1, 2, 3] + evens)
        if not last:
            send_pair(w + 1, 0)
        for i, p in enumerate(order):
            if i == (1 if last else 2):
                pull(w, odds)
            settle(w, p)
            stage(w, p)
            if not last and i == 1:
                combine(w + 1)
            if last and i == len(order) - 2:
                def add(k, acc):
                    tell(k).wait_recv()
                    return acc + lw[k]
                lws[0] = lax.fori_loop(1, chips, add, lw[0])
                pair_sum.start()

    pair_sum.wait()
    packed = lws[0, 0:1, :] + lws[1, 0:1, :]
    row = packed[:, 0:walkers]
    for j in range(1, pack):
        row = row + packed[:, j * walkers:(j + 1) * walkers]
    per = walkers // n
    lane = lax.broadcasted_iota(jnp.int32, (1, walkers), 1)
    spot = lax.broadcasted_iota(jnp.int32, (8, 128), 1)
    mine = jnp.zeros((8, 128), jnp.float32)
    for j in range(per):
        one = jnp.sum(jnp.where(lane == me * per + j, row, 0.0), axis=1, keepdims=True)
        mine = jnp.where(spot == j, one, mine)
    logw[...] = mine / math.sqrt(total)

    for w in range(waves):
        d2d(w, 0).wait_send()
        forward(w, 0).wait_send()

        def drain_near(k, c, w=w):
            near(w, k).wait_send()
            return c

        def drain_far(k, c, w=w):
            far(w, k).wait_send()
            return c

        def drain(k, c, w=w):
            d2d(w, k).wait_send()
            spread(w, k).wait_send()
            forward(w, k).wait_send()
            return c

        lax.fori_loop(1, 4, drain_near, 0)
        lax.fori_loop(4, chips, drain_far, 0)
        lax.fori_loop(1, chips, drain, 0)

    def drain_tell(k, c):
        tell(k).wait_send()
        return c

    lax.fori_loop(1, chips, drain_tell, 0)


def hand_over(pot, logw, pot_out, logw_out):
    pot_out[...] = pot[...]
    logw_out[...] = logw[0:1, 0:logw_out.shape[0]].reshape(logw_out.shape)


def solution(mesh):
    n = mesh.shape["chol"]

    def per_device(green, factors, noise):
        walkers, cols = green.shape
        total = factors.shape[0]
        chips = n // 2
        nv = total // n
        pack = max(1, 128 // walkers)
        waves = 2 if nv % (32 * pack) == 0 else 1
        half, lanes = nv // waves // pack, walkers * pack
        vmem = pl.BlockSpec(memory_space=pltpu.VMEM)
        hbm = pl.BlockSpec(memory_space=pltpu.HBM)
        dma = pltpu.SemaphoreType.DMA
        block = (waves * chips, half, lanes)
        pot, logw = pl.pallas_call(
            functools.partial(kernel, n, pack, waves),
            out_shape=(pltpu.VMEM((walkers, cols), jnp.float32), pltpu.VMEM((8, 128), jnp.float32)),
            in_specs=[hbm, hbm, hbm],
            out_specs=(vmem, vmem),
            scratch_shapes=[
                pltpu.VMEM(green.shape, jnp.bfloat16),
                pltpu.VMEM(noise.shape, jnp.float32),
                pltpu.VMEM(factors.shape, jnp.bfloat16),
                pltpu.VMEM((waves * chips, 2, half, lanes), jnp.float32),
                pltpu.VMEM(block, jnp.float32),
                pltpu.VMEM(block, jnp.float32),
                pltpu.VMEM(block, jnp.float32),
                pltpu.VMEM(block, jnp.bfloat16),
                pltpu.VMEM(block, jnp.bfloat16),
                pltpu.VMEM((waves, chips, 2, half, lanes), jnp.bfloat16),
                pltpu.VMEM((waves, half, lanes), jnp.float32),
                pltpu.VMEM((walkers, 4 * (nv // waves)), jnp.bfloat16),
                pltpu.VMEM((chips, 8, lanes), jnp.float32),
                pltpu.VMEM((2, 8, lanes), jnp.float32),
                dma((2,)), dma((4, waves * chips // 2)),
            ] + [dma((waves * chips,))] * 4 + [dma((waves, chips))] * 4 + [dma((chips,))] * 2 + [dma, dma],
            compiler_params=pltpu.CompilerParams(
                collective_id=0, has_side_effects=True, vmem_limit_bytes=58 * 2**20),
        )(green, factors, noise)
        return pl.pallas_call(
            hand_over,
            out_shape=(jax.ShapeDtypeStruct((walkers, cols), jnp.float32),
                       jax.ShapeDtypeStruct((walkers // n,), jnp.float32)),
            in_specs=[vmem, vmem],
            out_specs=(vmem, vmem),
            compiler_params=pltpu.CompilerParams(vmem_limit_bytes=4 * 2**20),
        )(pot, logw)

    return jax.shard_map(
        per_device,
        mesh=mesh,
        in_specs=(P("groups", "chol"), P(None, "chol"), P("groups", "chol")),
        out_specs=(P("groups", "chol"), P(("groups", "chol"))),
        check_vma=False,
    )
```

time: 49.3 us -> 39.9 us (0.81)
  Pallas kernels: 44.9 us -> 39.1 us
  local copies, waits for them, and re-layouts: 3.38 us -> 0 us
    pallas_call x1 -> x2, Pallas kernels: 44.9 us -> 39.1 us  [the longest x1 38.1 us: per_device(): pl.pallas_call(functools.partial(kernel, n, pack, waves), out_shape=(pltp...]
    unnamed x2 -> x0, local copies, waits for them, and re-layouts: 3.38 us -> none
where the time goes in v2:
time: 39.9 us; the launch traced here: 39.8 us
  Pallas kernels  39.1 us (98%)
  between operations  0.64 us (2%)
    pallas_call x1, Pallas kernels, per_device(): pl.pallas_call(functools.partial(kernel, n, pack, waves), out_shape=(pltp...  38.1 us
    pallas_call x1, Pallas kernels, per_device(): pl.pallas_call(hand_over, out_shape=(jax.ShapeDtypeStruct((walkers, cols)...  1.04 us

profile of v2, /device:TPU:0, one launch (start us, length us, event | category | flops | bytes accessed | tf_op | source)
XLA Modules:
  0.0 39.8 jit_solution(11434536807024118538)
XLA Ops:
  0.6 38.1 %shard_map.50 = (f32[64,4096]{1,0:T(8,128)S(1)}, f32[8,128]{1,0:T(8,128)S(1)}) custom-call(bf16[64,4096]{1,0:T(8,128)(2,1)} %green.1, bf16[5120,4096]{1,0:T(8,128)(2,1)} %factors.1, f32[64,320]{1,0:T(8,128)} %noise.1), custom_call_target="tpu_custom_call" | custom-call | tf_op jit(solution)/shard_map/pallas_call | solution.py:339
  38.7 1.0 %shard_map.51 = (f32[64,4096]{1,0:T(8,128)}, f32[4]{0:T(128)}) custom-call(f32[64,4096]{1,0:T(8,128)S(1)} %get-tuple-element.4.pot, f32[8,128]{1,0:T(8,128)S(1)} %get-tuple-element.5.logw), custom_call_target="tpu_custom_call" | custom-call | tf_op jit(solution)/shard_map/pallas_call | solution.py:364

commit v3 on v2

v3 whole, which is shorter than its diff:
```python
import functools
import math

import jax
import jax.numpy as jnp
from jax import lax
from jax.experimental import pallas as pl
from jax.experimental.pallas import tpu as pltpu
from jax.sharding import PartitionSpec as P

MESH = pl.DeviceIdType.MESH


def flip(a, b, bits):
    total = 0
    for bit in range(bits):
        x = lax.rem(lax.div(a, 2**bit), 2)
        y = lax.rem(lax.div(b, 2**bit), 2) if not isinstance(b, int) else (b >> bit) & 1
        total = total + (x + y - 2 * x * y) * 2**bit
    return total


def kernel(n, pack, waves, green, factors, noise, pot, logw,
           grn, nzi, fac, part, d2d_in, own, rs_out, rs_in, ag, nz, lhs, lw, lws,
           in_sem, fac_sem, ds, dr, rs, rr, gs, gr, fs, fr, ls, lr, ps, pr):
    chips = n // 2
    bits = chips.bit_length() - 1
    pairs = chips // 2
    total, cols = factors.shape
    nv = total // n
    nw = nv // waves
    half = nw // pack
    walkers = green.shape[0]
    deep = 4 * nw
    me = lax.axis_index("chol")
    chip, core = lax.div(me, 2), lax.rem(me, 2)
    other = 1 - core
    partner = chip * 2 + other

    def peer(k):
        return flip(chip, k, bits) * 2 + core

    def at(w, k):
        return w * chips + k

    def base(w, p):
        return pl.multiple_of((w * pairs + p) * deep, deep)

    def member(p, b):
        if isinstance(p, int):
            return p // 2 * 4 + p % 2 + 2 * b
        return lax.div(p, 2) * 4 + lax.rem(p, 2) + 2 * b

    def load(w, p, b, c):
        src = (flip(chip, member(p, b), bits) * 2 + c) * nv + w * nw
        return pltpu.make_async_copy(
            factors.at[pl.ds(pl.multiple_of(src, nw), nw), :],
            fac.at[pl.ds(pl.multiple_of(base(w, p) + (2 * b + c) * nw, nw), nw), :],
            fac_sem.at[w * pairs + p])

    green_in = pltpu.make_async_copy(green, grn, in_sem.at[0])
    noise_in = pltpu.make_async_copy(noise, nzi, in_sem.at[1])
    green_in.start()
    steps = waves * pairs

    def where(t):
        return lax.div(t, pairs), pairs - 1 - lax.rem(t, pairs)

    def start_load(t, c):
        w, p = where(t)
        for b in (0, 1):
            for e in range(2):
                load(w, p, b, e).start()
        return c

    start_load(0, 0)
    noise_in.start()
    lax.fori_loop(1, steps, start_load, 0)

    barrier = pltpu.get_barrier_semaphore()
    pl.semaphore_signal(barrier, inc=1, device_id={"chol": partner}, device_id_type=MESH)

    def greet(k, c):
        pl.semaphore_signal(barrier, inc=1, device_id={"chol": peer(k)}, device_id_type=MESH)
        return c

    lax.fori_loop(1, chips, greet, 0)

    def remote(src, dst, s, r, to):
        return pltpu.make_async_remote_copy(
            src_ref=src, dst_ref=dst, send_sem=s, recv_sem=r,
            device_id={"chol": to}, device_id_type=MESH)

    def arrived(ref, sem):
        pltpu.make_async_copy(ref, ref, sem).wait()

    def blocks_of(count):
        return rs_in.at[pl.ds(0, count)]

    def d2d(w, p, b):
        q = at(w, member(p, b))
        return remote(part.at[q, other], d2d_in.at[q], ds, dr.at[w * pairs + p], partner)

    def send(w, k, to, group):
        q = at(w, k)
        return remote(rs_out.at[q], rs_in.at[q], rs, rr.at[w, group], peer(to))

    def pack_rows(o):
        rows = [o[j * half:(j + 1) * half] for j in range(pack)]
        return jnp.concatenate(rows, axis=1) if pack > 1 else rows[0]

    def product(w, p):
        arrived(fac.at[pl.ds(base(w, p), deep), :], fac_sem.at[w * pairs + p])
        o = lax.dot_general(fac[pl.ds(base(w, p), deep), :], grn[...], (((1,), (1,)), ((), ())),
                            preferred_element_type=jnp.float32)
        for b in range(2):
            for e in range(2):
                part[at(w, member(p, b)), e] = pack_rows(o[(2 * b + e) * nw:(2 * b + e + 1) * nw])

    def swap(w, p):
        for b in (1, 0):
            d2d(w, p, b).start()

    def swapped(w, p):
        arrived(d2d_in.at[pl.ds(0, 2)], dr.at[w * pairs + p])

    def reduced(w, k):
        q = at(w, k)
        return part[q, core] + d2d_in[q]

    def push(w, k, to, group, value):
        rs_out[at(w, k)] = value.astype(jnp.bfloat16)
        send(w, k, to, group).start()

    def service(w, p):
        @pl.when((p >= 2) & (lax.rem(p, 2) == 1))
        def _():
            swapped(w, p)
            for b in (1, 0):
                k = member(p, b)
                push(w, k, 1, lax.div(p, 2), reduced(w, k))

        @pl.when(p == 1)
        def _():
            swapped(w, p)
            for k in (3, 1):
                push(w, k, k, 0, reduced(w, k))

    def service_far(w, p):
        @pl.when((p >= 2) & (lax.rem(p, 2) == 0))
        def _():
            swapped(w, p)
            arrived(blocks_of(2), rr.at[w, lax.div(p, 2)])
            for b in (1, 0):
                k = member(p, b)
                push(w, k, k, 0, reduced(w, k) + rs_in[at(w, k + 1)].astype(jnp.float32))

    def service_last(w):
        swapped(w, 0)
        push(w, 2, 2, 0, reduced(w, 2))
        own[w] = reduced(w, 0)

    evens = list(range(4, chips, 2))
    odds = [k + 1 for k in evens]

    def got(k):
        return 0 if k < 4 else 1 if k % 2 else k // 2

    def spread(w, k):
        return remote(ag.at[w, 0, core], ag.at[w, k, core], gs, gr.at[w, got(k)], peer(k))

    def relay(w, k):
        return remote(ag.at[w, k - 1, core], ag.at[w, k, core], gs, gr.at[w, got(k)], peer(1))

    def forward(w, k):
        return remote(ag.at[w, k, core], ag.at[w, k, core], fs, fr.at[w, k // 4 * 2 + k % 2], partner)

    def tell(k):
        return remote(lw.at[0], lw.at[k], ls, lr, peer(k))

    pair_sum = remote(lws.at[0], lws.at[1], ps, pr, partner)
    order = range(pairs)

    def combine(w):
        forces = own[w]
        arrived(blocks_of(3 + len(evens)), rr.at[w, 0])
        for k in evens + [1, 2, 3]:
            forces = forces + rs_in[at(w, k)].astype(jnp.float32)
        capped = jnp.tanh(forces)
        fields = nz[w] - capped
        ag[w, 0, core] = fields.astype(jnp.bfloat16)
        for k in evens[::-1] + [2, 3, 1]:
            spread(w, k).start()
        forward(w, 0).start()
        row = jnp.sum(fields * capped - 0.5 * capped * capped, axis=0, keepdims=True)
        row = jnp.broadcast_to(row, lw.shape[1:])
        lw[0] = row if w == 0 else lw[0] + row
        if w == waves - 1:
            def start_tell(k, c):
                tell(k).start()
                return c

            lax.fori_loop(1, chips, start_tell, 0)

    def pull_near(w):
        arrived(blocks_of(3), gr.at[w, 0])
        for k in (1, 2, 3):
            forward(w, k).start()

    def pull_evens(w):
        for k in evens:
            arrived(blocks_of(1), gr.at[w, got(k)])
            relay(w, k + 1).start()
            forward(w, k).start()

    def pull_odds(w):
        if odds:
            arrived(blocks_of(len(odds)), gr.at[w, 1])
        for k in odds:
            forward(w, k).start()

    def settle(w, p):
        arrived(blocks_of(2), fr.at[w, p])

    def stage(w, p):
        blocks = []
        for b in range(2):
            for e in range(2):
                block = ag[w, member(p, b), e]
                for j in range(pack):
                    blocks.append(block[:, j * walkers:(j + 1) * walkers])
        lhs[...] = jnp.concatenate(blocks, axis=0).T
        value = jnp.dot(lhs[...], fac[pl.ds(base(w, p), deep), :], preferred_element_type=jnp.float32)
        pot[...] = value if w == 0 and p == order[0] else pot[...] + value

    green_in.wait()

    def step(t, c):
        w, p = where(t)
        product(w, p)

        @pl.when(t == 0)
        def _():
            pl.semaphore_wait(barrier, chips)

        swap(w, p)

        @pl.when(t > 1)
        def _():
            service_far(*where(t - 2))

        @pl.when(t > 0)
        def _():
            service(*where(t - 1))

        for v in range(waves - 1):
            @pl.when(t == (v + 1) * pairs)
            def _(v=v):
                service_last(v)

        @pl.when(t == 0)
        def _():
            noise_in.wait()
            turned = nzi[...].T
            for v in range(waves):
                nz[v] = pack_rows(turned[v * nw:(v + 1) * nw])

        for v in range(waves - 1):
            @pl.when(t == (v + 1) * pairs + pairs // 2)
            def _(v=v):
                combine(v)
        return c

    lax.fori_loop(0, steps, step, 0)
    def settle_weights():
        arrived(lw.at[pl.ds(1, chips - 1)], lr)
        acc = lw[0]
        for k in range(1, chips):
            acc = acc + lw[k]
        lws[0] = acc
        pair_sum.start()

    def write_weights():
        pair_sum.wait()
        packed = lws[0, 0:1, :] + lws[1, 0:1, :]
        row = packed[:, 0:walkers]
        for j in range(1, pack):
            row = row + packed[:, j * walkers:(j + 1) * walkers]
        per = walkers // n
        lane = lax.broadcasted_iota(jnp.int32, (1, walkers), 1)
        spot = lax.broadcasted_iota(jnp.int32, (8, 128), 1)
        mine = jnp.zeros((8, 128), jnp.float32)
        for j in range(per):
            one = jnp.sum(jnp.where(lane == me * per + j, row, 0.0), axis=1, keepdims=True)
            mine = jnp.where(spot == j, one, mine)
        logw[...] = mine / math.sqrt(total)

    if waves == 1:
        service_last(0)
        combine(0)
    for w in range(waves):
        last = w == waves - 1
        if last:
            pull_evens(w)
            pull_near(w)
        else:
            pull_near(w)
            service_last(w + 1)
            pull_evens(w)
        for i, p in enumerate(order):
            settle(w, p)
            stage(w, p)
            if not last and i == 1:
                combine(w + 1)
            if last and i == 0:
                settle_weights()
            if i == (0 if last else 1):
                pull_odds(w)
            if last and i == len(order) - 2:
                write_weights()

    arrived(d2d_in, ds)
    arrived(blocks_of(waves * (chips - 1)), rs)
    arrived(blocks_of(waves * (chips - 1)), gs)
    arrived(blocks_of(waves * chips), fs)
    arrived(lw.at[pl.ds(1, chips - 1)], ls)


def hand_over(pot, logw, pot_out, logw_out):
    pot_out[...] = pot[...]
    logw_out[...] = logw[0:1, 0:logw_out.shape[0]].reshape(logw_out.shape)


def solution(mesh):
    n = mesh.shape["chol"]

    def per_device(green, factors, noise):
        walkers, cols = green.shape
        total = factors.shape[0]
        chips = n // 2
        nv = total // n
        pack = max(1, 128 // walkers)
        waves = 2 if nv % (32 * pack) == 0 else 1
        half, lanes = nv // waves // pack, walkers * pack
        vmem = pl.BlockSpec(memory_space=pltpu.VMEM)
        hbm = pl.BlockSpec(memory_space=pltpu.HBM)
        dma = pltpu.SemaphoreType.DMA
        block = (waves * chips, half, lanes)
        pot, logw = pl.pallas_call(
            functools.partial(kernel, n, pack, waves),
            out_shape=(pltpu.VMEM((walkers, cols), jnp.float32), pltpu.VMEM((8, 128), jnp.float32)),
            in_specs=[hbm, hbm, hbm],
            out_specs=(vmem, vmem),
            scratch_shapes=[
                pltpu.VMEM(green.shape, jnp.bfloat16),
                pltpu.VMEM(noise.shape, jnp.float32),
                pltpu.VMEM(factors.shape, jnp.bfloat16),
                pltpu.VMEM((waves * chips, 2, half, lanes), jnp.float32),
                pltpu.VMEM(block, jnp.float32),
                pltpu.VMEM((waves, half, lanes), jnp.float32),
                pltpu.VMEM(block, jnp.bfloat16),
                pltpu.VMEM(block, jnp.bfloat16),
                pltpu.VMEM((waves, chips, 2, half, lanes), jnp.bfloat16),
                pltpu.VMEM((waves, half, lanes), jnp.float32),
                pltpu.VMEM((walkers, 4 * (nv // waves)), jnp.bfloat16),
                pltpu.VMEM((chips, 8, lanes), jnp.float32),
                pltpu.VMEM((2, 8, lanes), jnp.float32),
                dma((2,)), dma((waves * chips // 2,)),
                dma, dma((waves * chips // 2,)), dma, dma((waves, chips // 4)),
                dma, dma((waves, chips // 2)), dma, dma((waves, chips // 2)),
                dma, dma, dma, dma,
            ],
            compiler_params=pltpu.CompilerParams(
                collective_id=0, has_side_effects=True, vmem_limit_bytes=58 * 2**20),
        )(green, factors, noise)
        return pl.pallas_call(
            hand_over,
            out_shape=(jax.ShapeDtypeStruct((walkers, cols), jnp.float32),
                       jax.ShapeDtypeStruct((walkers // n,), jnp.float32)),
            in_specs=[vmem, vmem],
            out_specs=(vmem, vmem),
            compiler_params=pltpu.CompilerParams(vmem_limit_bytes=4 * 2**20),
        )(pot, logw)

    return jax.shard_map(
        per_device,
        mesh=mesh,
        in_specs=(P("groups", "chol"), P(None, "chol"), P("groups", "chol")),
        out_specs=(P("groups", "chol"), P(("groups", "chol"))),
        check_vma=False,
    )
```

time: 39.9 us -> 37.8 us (0.947)
  Pallas kernels: 39.1 us -> 37 us
    pallas_call x1, Pallas kernels: 38.1 us -> 36 us  [per_device(): pl.pallas_call(functools.partial(kernel, n, pack, waves), out_shape=(pltp...]
where the time goes in v3:
time: 37.8 us; the launch traced here: 37.7 us
  Pallas kernels  37 us (98%)
  between operations  0.64 us (2%)
    pallas_call x1, Pallas kernels, per_device(): pl.pallas_call(functools.partial(kernel, n, pack, waves), out_shape=(pltp...  36 us
    pallas_call x1, Pallas kernels, per_device(): pl.pallas_call(hand_over, out_shape=(jax.ShapeDtypeStruct((walkers, cols)...  1.04 us

profile of v3, /device:TPU:0, one launch (start us, length us, event | category | flops | bytes accessed | tf_op | source)
XLA Modules:
  0.0 37.7 jit_solution(2471519002198469120)
XLA Ops:
  0.6 36.0 %shard_map.50 = (f32[64,4096]{1,0:T(8,128)S(1)}, f32[8,128]{1,0:T(8,128)S(1)}) custom-call(bf16[64,4096]{1,0:T(8,128)(2,1)} %green.1, bf16[5120,4096]{1,0:T(8,128)(2,1)} %factors.1, f32[64,320]{1,0:T(8,128)} %noise.1), custom_call_target="tpu_custom_call" | custom-call | tf_op jit(solution)/shard_map/pallas_call | solution.py:349
  36.6 1.0 %shard_map.51 = (f32[64,4096]{1,0:T(8,128)}, f32[4]{0:T(128)}) custom-call(f32[64,4096]{1,0:T(8,128)S(1)} %get-tuple-element.4.pot, f32[8,128]{1,0:T(8,128)S(1)} %get-tuple-element.5.logw), custom_call_target="tpu_custom_call" | custom-call | tf_op jit(solution)/shard_map/pallas_call | solution.py:376

commit v4 on v3

--- a/solution.py
+++ b/solution.py
@@ -189,7 +189,7 @@
         capped = jnp.tanh(forces)
         fields = nz[w] - capped
         ag[w, 0, core] = fields.astype(jnp.bfloat16)
-        for k in evens[::-1] + [2, 3, 1]:
+        for k in evens[::-1] + [2, 3, 1] if w == waves - 1 else [2, 3, 1] + evens[::-1]:
             spread(w, k).start()
         forward(w, 0).start()
         row = jnp.sum(fields * capped - 0.5 * capped * capped, axis=0, keepdims=True)
@@ -310,7 +310,7 @@
         for i, p in enumerate(order):
             settle(w, p)
             stage(w, p)
-            if not last and i == 1:
+            if not last and i == 0:
                 combine(w + 1)
             if last and i == 0:
                 settle_weights()

time: 37.8 us -> 36.3 us (0.960)
  Pallas kernels: 37 us -> 35.5 us
    pallas_call x1, Pallas kernels: 36 us -> 34.5 us  [per_device(): pl.pallas_call(functools.partial(kernel, n, pack, waves), out_shape=(pltp...]
where the time goes in v4:
time: 36.3 us; the launch traced here: 36.2 us
  Pallas kernels  35.5 us (98%)
  between operations  0.64 us (2%)
    pallas_call x1, Pallas kernels, per_device(): pl.pallas_call(functools.partial(kernel, n, pack, waves), out_shape=(pltp...  34.5 us
    pallas_call x1, Pallas kernels, per_device(): pl.pallas_call(hand_over, out_shape=(jax.ShapeDtypeStruct((walkers, cols)...  1.04 us

profile of v4, /device:TPU:0, one launch (start us, length us, event | category | flops | bytes accessed | tf_op | source)
XLA Modules:
  0.0 36.2 jit_solution(8143036315444951179)
XLA Ops:
  0.6 34.5 %shard_map.50 = (f32[64,4096]{1,0:T(8,128)S(1)}, f32[8,128]{1,0:T(8,128)S(1)}) custom-call(bf16[64,4096]{1,0:T(8,128)(2,1)} %green.1, bf16[5120,4096]{1,0:T(8,128)(2,1)} %factors.1, f32[64,320]{1,0:T(8,128)} %noise.1), custom_call_target="tpu_custom_call" | custom-call | tf_op jit(solution)/shard_map/pallas_call | solution.py:349
  35.1 1.0 %shard_map.51 = (f32[64,4096]{1,0:T(8,128)}, f32[4]{0:T(128)}) custom-call(f32[64,4096]{1,0:T(8,128)S(1)} %get-tuple-element.4.pot, f32[8,128]{1,0:T(8,128)S(1)} %get-tuple-element.5.logw), custom_call_target="tpu_custom_call" | custom-call | tf_op jit(solution)/shard_map/pallas_call | solution.py:376

commit v5 on v4

--- a/solution.py
+++ b/solution.py
@@ -301,8 +301,8 @@
     for w in range(waves):
         last = w == waves - 1
         if last:
+            pull_near(w)
             pull_evens(w)
-            pull_near(w)
         else:
             pull_near(w)
             service_last(w + 1)
@@ -314,7 +314,7 @@
                 combine(w + 1)
             if last and i == 0:
                 settle_weights()
-            if i == (0 if last else 1):
+            if i == 1:
                 pull_odds(w)
             if last and i == len(order) - 2:
                 write_weights()

time: 36.3 us -> 35.5 us (0.978)
  Pallas kernels: 35.5 us -> 34.7 us
    pallas_call x1, Pallas kernels: 34.5 us -> 33.6 us  [per_device(): pl.pallas_call(functools.partial(kernel, n, pack, waves), out_shape=(pltp...]
where the time goes in v5:
time: 35.5 us; the launch traced here: 35.3 us
  Pallas kernels  34.7 us (98%)
  between operations  0.64 us (2%)
    pallas_call x1, Pallas kernels, per_device(): pl.pallas_call(functools.partial(kernel, n, pack, waves), out_shape=(pltp...  33.6 us
    pallas_call x1, Pallas kernels, per_device(): pl.pallas_call(hand_over, out_shape=(jax.ShapeDtypeStruct((walkers, cols)...  1.04 us

profile of v5, /device:TPU:0, one launch (start us, length us, event | category | flops | bytes accessed | tf_op | source)
XLA Modules:
  0.0 35.3 jit_solution(6500801121467467712)
XLA Ops:
  0.6 33.6 %shard_map.50 = (f32[64,4096]{1,0:T(8,128)S(1)}, f32[8,128]{1,0:T(8,128)S(1)}) custom-call(bf16[64,4096]{1,0:T(8,128)(2,1)} %green.1, bf16[5120,4096]{1,0:T(8,128)(2,1)} %factors.1, f32[64,320]{1,0:T(8,128)} %noise.1), custom_call_target="tpu_custom_call" | custom-call | tf_op jit(solution)/shard_map/pallas_call | solution.py:349
  34.3 1.0 %shard_map.51 = (f32[64,4096]{1,0:T(8,128)}, f32[4]{0:T(128)}) custom-call(f32[64,4096]{1,0:T(8,128)S(1)} %get-tuple-element.4.pot, f32[8,128]{1,0:T(8,128)S(1)} %get-tuple-element.5.logw), custom_call_target="tpu_custom_call" | custom-call | tf_op jit(solution)/shard_map/pallas_call | solution.py:376

commit v6 on v5

--- a/solution.py
+++ b/solution.py
@@ -73,8 +73,8 @@
                 load(w, p, b, e).start()
         return c
 
+    noise_in.start()
     start_load(0, 0)
-    noise_in.start()
     lax.fori_loop(1, steps, start_load, 0)
 
     barrier = pltpu.get_barrier_semaphore()
@@ -233,6 +233,10 @@
         value = jnp.dot(lhs[...], fac[pl.ds(base(w, p), deep), :], preferred_element_type=jnp.float32)
         pot[...] = value if w == 0 and p == order[0] else pot[...] + value
 
+    noise_in.wait()
+    turned = nzi[...].T
+    for v in range(waves):
+        nz[v] = pack_rows(turned[v * nw:(v + 1) * nw])
     green_in.wait()
 
     def step(t, c):
@@ -257,13 +261,6 @@
             @pl.when(t == (v + 1) * pairs)
             def _(v=v):
                 service_last(v)
-
-        @pl.when(t == 0)
-        def _():
-            noise_in.wait()
-            turned = nzi[...].T
-            for v in range(waves):
-                nz[v] = pack_rows(turned[v * nw:(v + 1) * nw])
 
         for v in range(waves - 1):
             @pl.when(t == (v + 1) * pairs + pairs // 2)

time: 35.5 us -> 35.3 us (level)
  no operation moved by 1% of the time
where the time goes in v6:
time: 35.3 us; the launch traced here: 35.1 us
  Pallas kernels  34.5 us (98%)
  between operations  0.64 us (2%)
    pallas_call x1, Pallas kernels, per_device(): pl.pallas_call(functools.partial(kernel, n, pack, waves), out_shape=(pltp...  33.5 us
    pallas_call x1, Pallas kernels, per_device(): pl.pallas_call(hand_over, out_shape=(jax.ShapeDtypeStruct((walkers, cols)...  1.04 us

profile of v6, /device:TPU:0, one launch (start us, length us, event | category | flops | bytes accessed | tf_op | source)
XLA Modules:
  0.0 35.1 jit_solution(1670760695941301003)
XLA Ops:
  0.6 33.5 %shard_map.50 = (f32[64,4096]{1,0:T(8,128)S(1)}, f32[8,128]{1,0:T(8,128)S(1)}) custom-call(bf16[64,4096]{1,0:T(8,128)(2,1)} %green.1, bf16[5120,4096]{1,0:T(8,128)(2,1)} %factors.1, f32[64,320]{1,0:T(8,128)} %noise.1), custom_call_target="tpu_custom_call" | custom-call | tf_op jit(solution)/shard_map/pallas_call | solution.py:346
  34.1 1.0 %shard_map.51 = (f32[64,4096]{1,0:T(8,128)}, f32[4]{0:T(128)}) custom-call(f32[64,4096]{1,0:T(8,128)S(1)} %get-tuple-element.4.pot, f32[8,128]{1,0:T(8,128)S(1)} %get-tuple-element.5.logw), custom_call_target="tpu_custom_call" | custom-call | tf_op jit(solution)/shard_map/pallas_call | solution.py:373
